TPU v7x, 32 devices: a whole 2x2x4 slice. The times are simulated.
32 devices in a mesh: dp: 4 (over y, x), blk: 8 (over z, core).
Axes of the slice: x: 2, y: 2, z: 4, core: 2. Of those that a mesh axis runs over, the one named last changes fastest.
Arguments:
- particles: float32 [1024, 1024], P('blk'), may hold values from -14 to 14
- data_rows: bfloat16 [16384, 1024], P('dp'), may hold values from -0.1875 to 0.1875
- labels: int32 [16384], P('dp'), may hold values from 0 to 1
Outputs:
- descent: float32 [1024, 1024], P('blk')
All inputs are finite; a program needn't handle non-finite values.
Results may differ from a plain program's by a relative error of at most 0.0045.
Values may be sent and summed in bfloat16 or wider, within the bound.
A program may use at most 64 MiB of HBM per device.

v0:
```python
import jax
import jax.numpy as jnp
from jax import lax
from jax.sharding import PartitionSpec as P

prior_var = 4.0


def pair_sums(left_x, left_s, right_x, right_s, inv_band):
    feature_count = left_x.shape[1]
    left_xf = left_x.astype(jnp.float32)
    left_sf = left_s.astype(jnp.float32)
    right_xf = right_x.astype(jnp.float32)
    right_sf = right_s.astype(jnp.float32)
    left_norm = jnp.sum(left_xf * left_xf, axis=1)
    right_norm = jnp.sum(right_xf * right_xf, axis=1)
    left_sx = jnp.sum(left_sf * left_xf, axis=1)
    right_sx = jnp.sum(right_sf * right_xf, axis=1)
    gram_xx = jnp.einsum("id,jd->ij", left_x, right_x, preferred_element_type=jnp.float32)
    gram_ss = jnp.einsum("id,jd->ij", left_s, right_s, preferred_element_type=jnp.float32)
    cross_dot = jnp.einsum(
        "id,jd->ij",
        jnp.concatenate([left_x, left_s], axis=1),
        jnp.concatenate([right_s, right_x], axis=1),
        preferred_element_type=jnp.float32,
    )
    distance = left_norm[:, None] + right_norm[None, :] - 2.0 * gram_xx
    kernel = jnp.exp(-0.5 * inv_band * distance)
    bracket = (
        gram_ss
        + inv_band * (left_sx[:, None] - cross_dot + right_sx[None, :])
        + feature_count * inv_band
        - inv_band * inv_band * distance
    )
    weighted_kernel = kernel * bracket
    kernel_sum = jnp.sum(kernel, axis=1)
    weighted_sum = jnp.sum(weighted_kernel, axis=1)
    both_rows = jnp.dot(
        kernel.astype(jnp.bfloat16),
        jnp.concatenate([right_x, right_s], axis=1),
        preferred_element_type=jnp.float32,
    )
    kernel_x = both_rows[:, :feature_count]
    kernel_s = both_rows[:, feature_count:]
    weighted_x = jnp.dot(
        weighted_kernel.astype(jnp.bfloat16), right_x, preferred_element_type=jnp.float32
    )
    return (kernel_sum, weighted_sum, kernel_x, kernel_s, weighted_x)


def forces(left_x, left_s, sums, inv_band, particle_count):
    kernel_sum, weighted_sum, kernel_x, kernel_s, weighted_x = sums
    left_xf = left_x.astype(jnp.float32)
    left_sf = left_s.astype(jnp.float32)
    spread = kernel_sum[:, None] * left_xf - kernel_x
    score_force = (kernel_s + inv_band * spread) / particle_count
    place_force = (
        -inv_band * (weighted_sum[:, None] * left_xf - weighted_x)
        + inv_band * (kernel_sum[:, None] * left_sf - kernel_s)
        - 2.0 * inv_band * inv_band * spread
    ) / particle_count
    return (score_force, place_force)


def empty_sums(rows_count, feature_count):
    flat_zero = jnp.zeros((rows_count,), jnp.float32)
    wide_zero = jnp.zeros((rows_count, feature_count), jnp.float32)
    return (flat_zero, flat_zero, wide_zero, wide_zero, wide_zero)


def pair_folder(left_x, left_s, inv_band, running, pieces):
    pair_parts = pair_sums(left_x, left_s, pieces[0], pieces[1], inv_band)
    return jax.tree.map(jnp.add, running, pair_parts)


def shards(particles, data_rows, labels):
    block_rows, feature_count = particles.shape
    groups_count = lax.axis_size("dp")
    particle_count = block_rows * lax.axis_size("blk")
    inv_band = 1.0 / feature_count
    x_low = particles.astype(jnp.bfloat16)
    logits = jnp.einsum("pd,md->pm", x_low, data_rows, preferred_element_type=jnp.float32)
    probability = jax.nn.sigmoid(logits)
    residual = (labels.astype(jnp.float32)[None, :] - probability).astype(jnp.bfloat16)
    curvature = probability * (1.0 - probability)
    partial_score = jnp.dot(residual, data_rows, preferred_element_type=jnp.float32)
    scores = lax.psum(partial_score, "dp") - particles / prior_var
    s_low = scores.astype(jnp.bfloat16)
    share_rows = block_rows // groups_count
    offset = lax.axis_index("dp") * share_rows
    left_x = lax.dynamic_slice_in_dim(x_low, offset, share_rows, 0)
    left_s = lax.dynamic_slice_in_dim(s_low, offset, share_rows, 0)
    sums = pair_folder(
        left_x,
        left_s,
        inv_band,
        empty_sums(share_rows, feature_count),
        (
            lax.all_gather(x_low, "blk", axis=0, tiled=True),
            lax.all_gather(s_low, "blk", axis=0, tiled=True),
        ),
    )
    score_force, place_force = forces(left_x, left_s, sums, inv_band, particle_count)
    full_force = lax.all_gather(score_force, "dp", axis=0, tiled=True)
    own_place = lax.dynamic_update_slice_in_dim(
        jnp.zeros((block_rows, feature_count), jnp.float32), place_force, offset, 0
    )
    projected = jnp.einsum(
        "pd,md->pm", full_force.astype(jnp.bfloat16), data_rows, preferred_element_type=jnp.float32
    )
    weighted_rows = (curvature * projected).astype(jnp.bfloat16)
    data_term = jnp.dot(weighted_rows, data_rows, preferred_element_type=jnp.float32)
    summed = lax.psum(data_term - own_place, "dp")
    return summed + full_force / prior_var


def solution(mesh):
    placed = (P("blk", None), P("dp", None), P("dp"))
    return jax.shard_map(
        shards, mesh=mesh, in_specs=placed, out_specs=P("blk", None), check_vma=False
    )
```

profile of v0, /device:TPU:0, one launch (start us, length us, event | category | flops | bytes accessed | tf_op | source)
XLA Modules:
  0.0 181.4 jit_solution(16980919114636974199)
XLA Ops:
  7.4 0.0 all-reduce.3.cloned.1.call-start
  7.4 0.7 convert_element_type.42
  8.1 1.1 convert_element_type.38
  9.2 0.0 copy-start
  9.2 6.5 %fusion.3 = f32[128,4096]{1,0:T(8,128)S(1)} fusion(bf16[128,1024]{1,0:T(8,128)(2,1)S(1)} %convert_element_type.38, bf16[4096,1024]{1,0:T(8,128)(2,1)} %param.4), kind=kOutput, calls=%fused_computation.7 | convolution fusion | flops 1075314688 | bytes 10747904 | tf_op jit(solution)/shard_map/pd,md->pm/dot_general | solution.py:82
  15.7 1.3 copy-done.2
  17.0 2.1 %fusion.32 = f32[128,1024]{1,0:T(8,128)} fusion(bf16[4096,1024]{1,0:T(8,128)(2,1)S(1)} %copy-done, f32[128,4096]{1,0:T(8,128)S(1)} %fusion.3, f32[4096]{0:T(1024)S(1)} %convert_element_type.42), kind=kOutput, calls=%fused_computation.36 | convolution fusion | flops 1074790400 | bytes 11026432 | tf_op jit(solution)/shard_map/dot_general | solution.py:86
  19.1 0.0 all-reduce.3.cloned.1.call-update
  19.2 0.0 all-gather.3.cloned.1.call-start
  19.2 0.5 all-gather.3.cloned.1.call-update
  19.7 0.0 all-gather.5.cloned.1.call-start
  19.8 47.6 %all-reduce.3.cloned.1.call-done = f32[128,1024]{1,0:T(8,128)} async-done(((f32[128,1024]{1,0:T(8,128)}), f32[128,1024]{1,0:T(8,128)}) %all-reduce.3.cloned.1.call-update) | async-done | bytes 524304 | tf_op jit(solution)/shard_map/psum | solution.py:87
  67.4 1.8 subtract_convert_fusion.2
  69.2 0.0 all-gather.5.cloned.1.call-update
  69.2 0.0 all-reduce.5.cloned.1.call-start
  69.3 1.0 fusion.40
  70.3 0.0 all-gather.3.cloned.1.call-done
  70.3 28.1 %all-gather.5.cloned.1.call-done = bf16[1024,1024]{1,0:T(8,128)(2,1)} async-done(((bf16[128,1024]{1,0:T(8,128)(2,1)}), bf16[1024,1024]{1,0:T(8,128)(2,1)}) %all-gather.5.cloned.1.call-update) | async-done | bytes 2097168 | tf_op jit(solution)/shard_map/all_gather | solution.py:100
  98.4 3.1 %fusion.5 = (f32[1024]{0:T(1024)S(1)}, f32[1024]{0:T(1024)S(1)}) fusion(bf16[1024,1024]{1,0:T(8,128)(2,1)} %all-gather.3.cloned.1.call-done, bf16[1024,1024]{1,0:T(8,128)(2,1)} %all-gather.5.cloned.1.call-done), kind=kLoop, calls=%fused_computation.9 | loop fusion | flops 6289408 | bytes 4202496 | tf_op jit(solution)/shard_map/reduce_sum | solution.py:18
  101.6 0.8 fusion.44
  102.4 0.7 copy-done.3
  103.1 0.8 fusion.6
  103.9 0.1 add_multiply_fusion
  104.0 10.0 %all_gather.11 = f32[128,1024]{1,0:T(8,128)S(1)} all-gather(f32[32,1024]{1,0:T(8,128)S(1)} %add_multiply_fusion), channel_id=1, replica_groups=mesh['dp'=4,'blk'=8] {'dp'}, dimensions={0}, use_global_device_ids=true | all-gather | bytes 655360 | tf_op jit(solution)/shard_map/all_gather | solution.py:104
  114.0 1.3 fusion.29
  115.4 0.8 fusion.53
  116.2 0.1 broadcast_in_dim.2
  116.3 0.5 fusion.18
  116.8 11.2 %convolution_subtract_fusion = f32[128,1024]{1,0:T(8,128)} fusion(f32[128,1024]{1,0:T(8,128)S(1)} %fusion.18, bf16[4096,1024]{1,0:T(8,128)(2,1)} %param.4, f32[128,4096]{1,0:T(8,128)} %copy-done.2, f32[128,1024]{1,0:T(8,128)S(1)} %all_gather.11), kind=kOutput, calls=%fused_computation.20 | convolution fusion | flops 2149842944 | bytes 12058624 | tf_op jit(solution)/shard_map/dot_general | solution.py:112
  128.0 0.0 all-reduce.5.cloned.1.call-update
  128.1 44.0 %all-reduce.5.cloned.1.call-done = f32[128,1024]{1,0:T(8,128)} async-done(((f32[128,1024]{1,0:T(8,128)}), f32[128,1024]{1,0:T(8,128)}) %all-reduce.5.cloned.1.call-update) | async-done | bytes 524304 | tf_op jit(solution)/shard_map/psum | solution.py:113
  172.0 1.9 %multiply_add_fusion = f32[128,1024]{1,0:T(8,128)} fusion(f32[128,1024]{1,0:T(8,128)} %all-reduce.5.cloned.1.call-done, f32[128,1024]{1,0:T(8,128)S(1)} %all_gather.11), kind=kLoop, calls=%fused_computation.38 | loop fusion | flops 262144 | bytes 1572864 | tf_op jit(solution)/shard_map/add | solution.py:114
  (9 shorter events, 0.0 us)
Async XLA Ops:
  7.4 60.0 %all-reduce.3.cloned.1.call-start = ((), (), s32[]{:S(2)}) async-start(), calls=%async_computation.1 | async-start | bytes 1048576 | tf_op jit(solution)/shard_map/psum | solution.py:87
  9.2 6.5 %copy-start.5 = (bf16[128,1024]{1,0:T(8,128)(2,1)}, bf16[128,1024]{1,0:T(8,128)(2,1)S(1)}, u32[]{:S(2)}) copy-start(bf16[128,1024]{1,0:T(8,128)(2,1)S(1)} %convert_element_type.38) | copy-start | bytes 786436
  9.2 7.9 %copy-start = (bf16[4096,1024]{1,0:T(8,128)(2,1)S(1)}, bf16[4096,1024]{1,0:T(8,128)(2,1)}, u32[]{:S(2)}) copy-start(bf16[4096,1024]{1,0:T(8,128)(2,1)} %param.4) | copy-start | bytes 25165828
  15.7 1.4 copy-start.2
  17.0 50.4 %copy-start.4 = (f32[128,1024]{1,0:T(8,128)S(1)}, f32[128,1024]{1,0:T(8,128)}, u32[]{:S(2)}) copy-start(f32[128,1024]{1,0:T(8,128)} %param.3) | copy-start | bytes 1572868
  19.2 51.2 %all-gather.3.cloned.1.call-start = ((), (), s32[]{:S(2)}) async-start(), calls=%async_computation | async-start | bytes 2359296 | tf_op jit(solution)/shard_map/all_gather | solution.py:99
  19.7 78.7 %all-gather.5.cloned.1.call-start = ((), (), s32[]{:S(2)}) async-start(), calls=%async_computation.2 | async-start | bytes 2359296 | tf_op jit(solution)/shard_map/all_gather | solution.py:100
  69.2 102.8 %all-reduce.5.cloned.1.call-start = ((), (), s32[]{:S(2)}) async-start(), calls=%async_computation.3 | async-start | bytes 1048576 | tf_op jit(solution)/shard_map/psum | solution.py:113
  70.3 31.2 %copy-start.1 = (bf16[1024,1024]{1,0:T(8,128)(2,1)S(1)}, bf16[1024,1024]{1,0:T(8,128)(2,1)}, u32[]{:S(2)}) copy-start(bf16[1024,1024]{1,0:T(8,128)(2,1)} %all-gather.3.cloned.1.call-done) | copy-start | bytes 6291460
  101.5 1.6 copy-start.3
Sparse Core Ops, SparseCore 0:
  19.3 48.0 all-reduce.2
  128.2 43.7 all-reduce.4
Sparse Core Ops, SparseCore 1:
  21.2 31.8 all-gather.2
  69.3 29.0 all-gather.4
where the time goes:
time: 182 us; the launch traced here: 181 us
  waiting for transfers between devices  120 us (66%)
  matrix products  24.2 us (13%)
  between operations  15 us (8%)
  blocking collectives  10 us (5%)
  other arithmetic  9.71 us (5%)
  local copies, waits for them, and re-layouts  2.14 us (1%)
    psum x1, waiting for transfers between devices, shards(): scores = lax.psum(partial_score, 'dp') - particles / prior_var  47.6 us
    psum x1, waiting for transfers between devices, shards(): summed = lax.psum(data_term - own_place, 'dp')  44 us
    all_gather x1, waiting for transfers between devices, shards(): lax.all_gather(s_low, 'blk', axis=0, tiled=True)  28.1 us
    dot_general x1, matrix products, shards(): jnp.dot(weighted_rows, data_rows, preferred_element_type=jnp.float32)  11.2 us
    all_gather x1, blocking collectives, shards(): full_force = lax.all_gather(score_force, 'dp', axis=0, tiled=True)  10 us
    dot_general x1, matrix products, shards(): jnp.einsum('pd,md->pm', x_low, data_rows, preferred_element_type=jnp.floa...  6.47 us
  transfers between devices with their start and end apart: 4, of which 3 were waited for; matrix products, arithmetic and copies ran while one was open for 2% of the time, Pallas kernels for 0%

commit v1 on v0

--- a/solution.py
+++ b/solution.py
@@ -110,7 +110,7 @@
     )
     weighted_rows = (curvature * projected).astype(jnp.bfloat16)
     data_term = jnp.dot(weighted_rows, data_rows, preferred_element_type=jnp.float32)
-    summed = lax.psum(data_term - own_place, "dp")
+    summed = jnp.sum(lax.all_gather(data_term - own_place, "dp"), axis=0)
     return summed + full_force / prior_var
 
 

time: 182 us -> 172 us (0.945)
  waiting for transfers between devices: 120 us -> 110 us
    psum x1 -> x0, waiting for transfers between devices: 44 us -> none  [shards(): summed = lax.psum(data_term - own_place, 'dp')]
    all_gather x0 -> x1, waiting for transfers between devices: none -> 33.8 us  [shards(): summed = jnp.sum(lax.all_gather(data_term - own_place, 'dp'), axis=0)]
where the time goes in v1:
time: 172 us
  waiting for transfers between devices  110 us (64%)
  matrix products  24.2 us (14%)
  between operations  15 us (9%)
  other arithmetic  10.5 us (6%)
  blocking collectives  10 us (6%)
  local copies, waits for them, and re-layouts  2.14 us (1%)
    psum x1, waiting for transfers between devices, shards(): scores = lax.psum(partial_score, 'dp') - particles / prior_var  47.6 us
    all_gather x1, waiting for transfers between devices, shards(): summed = jnp.sum(lax.all_gather(data_term - own_place, 'dp'), axis=0)  33.8 us
    all_gather x1, waiting for transfers between devices, shards(): lax.all_gather(s_low, 'blk', axis=0, tiled=True)  28.1 us
    dot_general x1, matrix products, shards(): jnp.dot(weighted_rows, data_rows, preferred_element_type=jnp.float32)  11.2 us
    all_gather x1, blocking collectives, shards(): full_force = lax.all_gather(score_force, 'dp', axis=0, tiled=True)  10 us
    dot_general x1, matrix products, shards(): jnp.einsum('pd,md->pm', x_low, data_rows, preferred_element_type=jnp.floa...  6.47 us
  transfers between devices with their start and end apart: 4, of which 3 were waited for; matrix products, arithmetic and copies ran while one was open for 2% of the time, Pallas kernels for 0%

profile of v1, /device:TPU:0, one launch (start us, length us, event | category | flops | bytes accessed | tf_op | source)
XLA Modules:
  0.0 171.9 jit_solution(755957474403363872)
XLA Ops:
  7.4 0.7 convert_element_type.42
  8.1 1.1 convert_element_type.38
  9.2 0.0 copy-start
  9.2 6.5 %fusion.3 = f32[128,4096]{1,0:T(8,128)S(1)} fusion(bf16[128,1024]{1,0:T(8,128)(2,1)S(1)} %convert_element_type.38, bf16[4096,1024]{1,0:T(8,128)(2,1)} %param.4), kind=kOutput, calls=%fused_computation.7 | convolution fusion | flops 1075314688 | bytes 10747904 | tf_op jit(solution)/shard_map/pd,md->pm/dot_general | solution.py:82
  15.7 1.3 copy-done.2
  17.0 2.1 %fusion.32 = f32[128,1024]{1,0:T(8,128)} fusion(bf16[4096,1024]{1,0:T(8,128)(2,1)S(1)} %copy-done, f32[128,4096]{1,0:T(8,128)S(1)} %fusion.3, f32[4096]{0:T(1024)S(1)} %convert_element_type.42), kind=kOutput, calls=%fused_computation.36 | convolution fusion | flops 1074790400 | bytes 11026432 | tf_op jit(solution)/shard_map/dot_general | solution.py:86
  19.1 0.0 all-reduce.2.cloned.1.call-update
  19.2 0.0 all-gather.5.cloned.1.call-start
  19.2 0.5 all-gather.5.cloned.1.call-update
  19.7 0.0 all-gather.7.cloned.1.call-start
  19.8 47.6 %all-reduce.2.cloned.1.call-done = f32[128,1024]{1,0:T(8,128)} async-done(((f32[128,1024]{1,0:T(8,128)}), f32[128,1024]{1,0:T(8,128)}) %all-reduce.2.cloned.1.call-update) | async-done | bytes 524304 | tf_op jit(solution)/shard_map/psum | solution.py:87
  67.4 1.8 %subtract_convert_fusion.2 = bf16[128,1024]{1,0:T(8,128)(2,1)} fusion(f32[128,1024]{1,0:T(8,128)} %all-reduce.2.cloned.1.call-done, f32[128,1024]{1,0:T(8,128)S(1)} %copy-done.4), kind=kLoop, calls=%fused_computation.39 | loop fusion | flops 393216 | bytes 1310720 | tf_op jit(solution)/shard_map/convert_element_type | solution.py:88
  69.2 0.0 all-gather.7.cloned.1.call-update
  69.2 0.0 all-gather.9.cloned.1.call-start
  69.3 1.0 fusion.40
  70.3 0.0 all-gather.5.cloned.1.call-done
  70.3 28.1 %all-gather.7.cloned.1.call-done = bf16[1024,1024]{1,0:T(8,128)(2,1)} async-done(((bf16[128,1024]{1,0:T(8,128)(2,1)}), bf16[1024,1024]{1,0:T(8,128)(2,1)}) %all-gather.7.cloned.1.call-update) | async-done | bytes 2097168 | tf_op jit(solution)/shard_map/all_gather | solution.py:100
  98.4 3.1 %fusion.5 = (f32[1024]{0:T(1024)S(1)}, f32[1024]{0:T(1024)S(1)}) fusion(bf16[1024,1024]{1,0:T(8,128)(2,1)} %all-gather.5.cloned.1.call-done, bf16[1024,1024]{1,0:T(8,128)(2,1)} %all-gather.7.cloned.1.call-done), kind=kLoop, calls=%fused_computation.9 | loop fusion | flops 6289408 | bytes 4202496 | tf_op jit(solution)/shard_map/reduce_sum | solution.py:18
  101.6 0.8 fusion.44
  102.4 0.7 copy-done.3
  103.1 0.8 fusion.6
  103.9 0.1 add_multiply_fusion
  104.0 10.0 %all_gather.17 = f32[128,1024]{1,0:T(8,128)S(1)} all-gather(f32[32,1024]{1,0:T(8,128)S(1)} %add_multiply_fusion), channel_id=1, replica_groups=mesh['dp'=4,'blk'=8] {'dp'}, dimensions={0}, use_global_device_ids=true | all-gather | bytes 655360 | tf_op jit(solution)/shard_map/all_gather | solution.py:104
  114.0 1.3 fusion.29
  115.4 0.8 fusion.53
  116.2 0.1 broadcast_in_dim.2
  116.3 0.5 fusion.18
  116.8 11.2 %convolution_subtract_fusion = f32[128,1024]{1,0:T(8,128)} fusion(f32[128,1024]{1,0:T(8,128)S(1)} %fusion.18, bf16[4096,1024]{1,0:T(8,128)(2,1)} %param.4, f32[128,4096]{1,0:T(8,128)} %copy-done.2, f32[128,1024]{1,0:T(8,128)S(1)} %all_gather.17), kind=kOutput, calls=%fused_computation.20 | convolution fusion | flops 2149842944 | bytes 12058624 | tf_op jit(solution)/shard_map/dot_general | solution.py:112
  128.0 0.0 all-gather.9.cloned.1.call-update
  128.1 33.8 %all-gather.9.cloned.1.call-done = f32[512,1024]{1,0:T(8,128)} async-done(((f32[128,1024]{1,0:T(8,128)}), f32[512,1024]{1,0:T(8,128)}) %all-gather.9.cloned.1.call-update) | async-done | bytes 2097168 | tf_op jit(solution)/shard_map/all_gather | solution.py:113
  161.8 1.8 %reduce_sum.69 = f32[128,1024]{1,0:T(8,128)S(1)} reduce(f32[4,128,1024]{2,1,0:T(8,128)} %bitcast.12, f32[]{:T(128)} %constant.7.clone.1), dimensions={0}, to_apply=%region_7.0 | reduce | flops 393216 | bytes 2621444 | tf_op jit(solution)/shard_map/reduce_sum | solution.py:113
  163.6 0.9 multiply_add_fusion
  (10 shorter events, 0.0 us)
Async XLA Ops:
  7.4 60.0 %all-reduce.2.cloned.1.call-start = ((), (), s32[]{:S(2)}) async-start(), calls=%async_computation.1 | async-start | bytes 1048576 | tf_op jit(solution)/shard_map/psum | solution.py:87
  9.2 6.5 %copy-start.5 = (bf16[128,1024]{1,0:T(8,128)(2,1)}, bf16[128,1024]{1,0:T(8,128)(2,1)S(1)}, u32[]{:S(2)}) copy-start(bf16[128,1024]{1,0:T(8,128)(2,1)S(1)} %convert_element_type.38) | copy-start | bytes 786436
  9.2 7.9 %copy-start = (bf16[4096,1024]{1,0:T(8,128)(2,1)S(1)}, bf16[4096,1024]{1,0:T(8,128)(2,1)}, u32[]{:S(2)}) copy-start(bf16[4096,1024]{1,0:T(8,128)(2,1)} %param.4) | copy-start | bytes 25165828
  15.7 1.4 copy-start.2
  17.0 50.4 %copy-start.4 = (f32[128,1024]{1,0:T(8,128)S(1)}, f32[128,1024]{1,0:T(8,128)}, u32[]{:S(2)}) copy-start(f32[128,1024]{1,0:T(8,128)} %param.3) | copy-start | bytes 1572868
  19.2 51.2 %all-gather.5.cloned.1.call-start = ((), (), s32[]{:S(2)}) async-start(), calls=%async_computation | async-start | bytes 2359296 | tf_op jit(solution)/shard_map/all_gather | solution.py:99
  19.7 78.7 %all-gather.7.cloned.1.call-start = ((), (), s32[]{:S(2)}) async-start(), calls=%async_computation.2 | async-start | bytes 2359296 | tf_op jit(solution)/shard_map/all_gather | solution.py:100
  69.2 92.6 %all-gather.9.cloned.1.call-start = ((), (), s32[]{:S(2)}) async-start(), calls=%async_computation.3 | async-start | bytes 2621440 | tf_op jit(solution)/shard_map/all_gather | solution.py:113
  70.3 31.2 %copy-start.1 = (bf16[1024,1024]{1,0:T(8,128)(2,1)S(1)}, bf16[1024,1024]{1,0:T(8,128)(2,1)}, u32[]{:S(2)}) copy-start(bf16[1024,1024]{1,0:T(8,128)(2,1)} %all-gather.5.cloned.1.call-done) | copy-start | bytes 6291460
  101.5 1.6 copy-start.3
Sparse Core Ops, SparseCore 0:
  19.3 48.0 all-reduce.1
  128.2 33.5 all-gather.8
Sparse Core Ops, SparseCore 1:
  21.2 31.8 all-gather.4
  69.3 29.0 all-gather.6
